TPU v7x, 32 devices: a whole 2x2x4 slice. The times are simulated.
32 devices in a mesh: slides: 2 (over y), row: 16 (over z, x, core).
Axes of the slice: x: 2, y: 2, z: 4, core: 2. Of those that a mesh axis runs over, the one named last changes fastest.
Arguments:
- slide_pixels: bfloat16 [2048, 16384], P(('slides', 'row')), parts along dimension 0, may hold values from -6 to 6
- tissue_mask: int32 [64, 8], P(('slides', 'row')), parts along dimension 0, may hold values from 0 to 1, as said below
- conv_weight: bfloat16 [3, 3, 64, 64], replicated, may hold values from -0.25 to 0.25
- conv_bias: bfloat16 [64], replicated, may hold values from -3 to 3
Outputs:
- packed_tiles: bfloat16 [256, 32, 2048], P(('slides', 'row')), parts along dimension 0
There are 2 independent parts, one for each index of `slides`. A program takes and returns all parts, laid end to end along the dimension named above; an argument that names none is the same for every part. Nothing has to cross between parts.
Inputs may be any that keep to these rules, and one draw needn't show every extreme that they name: `tissue_mask`: exactly 128 tiles hold tissue. For every s from 1 to 15, the first s * 2 tile rows hold s * 8 + e tissue tiles with e between 0 and 2; e = 2 occurs in every draw. For every such s, some column holds tissue in both tile row s * 2 - 1 and tile row s * 2.
All inputs are finite; a program needn't handle non-finite values.
Results may differ from a plain program's by a relative error of at most 0.001.
Values may be sent and summed in bfloat16 or wider, within the bound.
A program may use at most 64 MiB of HBM per device.

v0:
```python
import jax
import jax.numpy as jnp
from jax import lax
from jax.sharding import PartitionSpec as P

SLOTS = 8
SHIFT_MOST = 2


def extended(array, sides, width):
    for axis, dim in sides:
        size, length = (lax.axis_size(axis), array.shape[dim])
        up = [(i, (i + 1) % size) for i in range(size - 1)]
        down = [(j, i) for i, j in up]
        last = lax.slice_in_dim(array, length - width, length, axis=dim)
        initial = lax.slice_in_dim(array, 0, width, axis=dim)
        before = lax.ppermute(last, axis, up)
        after = lax.ppermute(initial, axis, down)
        array = jnp.concatenate([before, array, after], axis=dim)
    return array


def entering(part, axis, combine, identity):
    place = lax.axis_index(axis)
    gathered = lax.all_gather(part, axis)
    state = jnp.zeros_like(part) + jnp.asarray(identity, part.dtype)

    def one(step, state):
        return combine(state, lax.dynamic_index_in_dim(gathered, step, 0, False))

    return lax.fori_loop(0, place, one, state)


def passed_along(array, axis, by):
    length = lax.axis_size(axis)
    pairs = [(i, i + by) for i in range(length) if 0 <= i + by < length]
    return lax.ppermute(array, axis, pairs)


def add_counts(earlier, later):
    return earlier + later


def convolve(padded, conv_weight, conv_bias):
    tile_count = padded.shape[0]
    channels = conv_weight.shape[2]
    side = padded.shape[1] - 2
    pixels = padded.reshape(tile_count, side + 2, side + 2, channels)
    widened = jnp.concatenate(
        [pixels[:, :, 0:side], pixels[:, :, 1 : side + 1], pixels[:, :, 2 : side + 2]], axis=3
    )
    result = jnp.zeros((tile_count, side, side, channels), jnp.float32)
    for vertical in range(3):
        kernel = conv_weight[vertical].reshape(3 * channels, channels)
        result = result + jnp.einsum(
            "nhwk,ko->nhwo",
            widened[:, vertical : vertical + side],
            kernel,
            preferred_element_type=jnp.float32,
        )
    result = result + conv_bias.astype(jnp.float32)
    return result.astype(jnp.bfloat16).reshape(tile_count, side, side * channels)


def on_device(slide_pixels, tissue_mask, conv_weight, conv_bias):
    band_rows, grid_cols = tissue_mask.shape
    channels = conv_weight.shape[2]
    side = slide_pixels.shape[0] // band_rows
    tile_total = band_rows * grid_cols
    flat_mask = tissue_mask.reshape(tile_total)
    own_count = jnp.sum(flat_mask)
    blocks = slide_pixels.reshape(band_rows, side, grid_cols, side, channels)
    keeps = tissue_mask.astype(jnp.bfloat16)[:, None, :, None, None]
    masked = (blocks * keeps).reshape(band_rows * side, grid_cols * side * channels)
    haloed = extended(masked, (("row", 0),), 1)
    widened = haloed.reshape(band_rows * side + 2, grid_cols * side, channels)
    widened = jnp.pad(widened, ((0, 0), (1, 1), (0, 0)))
    pieces = []
    for tile_row in range(band_rows):
        for tile_col in range(grid_cols):
            window = widened[
                tile_row * side : tile_row * side + side + 2,
                tile_col * side : tile_col * side + side + 2,
            ]
            pieces.append(window.reshape(side + 2, (side + 2) * channels))
    padded_tiles = jnp.stack(pieces)
    device = lax.axis_index("row")
    earlier = entering(own_count.reshape(1), "row", add_counts, jnp.zeros((1,), jnp.int32))[0]
    order = jnp.argsort(1 - flat_mask, stable=True)
    first_rank = device * SLOTS

    def select(start, amount):
        ranks = start + jnp.arange(amount, dtype=jnp.int32)
        local = ranks - earlier
        present = (local >= 0) & (local < own_count)
        where_tile = jnp.take(order, jnp.clip(local, 0, tile_total - 1), axis=0)
        chosen = jnp.take(padded_tiles, where_tile, axis=0)
        return (chosen, present)

    kept, kept_live = select(first_rank, SLOTS)
    onward, onward_live = select(first_rank + SLOTS, SHIFT_MOST)
    upper = SLOTS - SHIFT_MOST

    def keep_live(values, live):
        return jnp.where(live[:, None, None], values, jnp.zeros_like(values))

    from_prev = passed_along(keep_live(onward, onward_live), "row", 1)
    owned = keep_live(kept, kept_live) + jnp.pad(from_prev, ((0, upper), (0, 0), (0, 0)))
    return convolve(owned, conv_weight, conv_bias)


def solution(mesh):
    return jax.shard_map(
        on_device,
        mesh=mesh,
        in_specs=(P(("slides", "row"), None), P(("slides", "row"), None), P(), P()),
        out_specs=P(("slides", "row"), None, None),
        check_vma=False,
    )
```

profile of v0, /device:TPU:26, one launch (start us, length us, event | category | flops | bytes accessed | tf_op | source)
XLA Modules:
  0.0 126.3 jit_solution(14673392390898853736)
XLA Ops:
  0.0 1.4 %fusion.18 = (s32[]{:T(128)}, bf16[2,8]{1,0:T(2,128)(2,1)S(1)}, s32[2,8]{1,0:T(2,128)S(1)}) fusion(s32[2,8]{1,0:T(2,128)} %param.7), kind=kLoop, calls=%fused_computation.72 | loop fusion | flops 47 | bytes 164 | tf_op jit(solution)/shard_map/reduce_sum | solution.py:71
  1.4 3.0 %mul.15 = bf16[2,32,8,32,64]{4,3,2,1,0:T(8,128)(2,1)} broadcast(bf16[2,8]{1,0:T(2,128)(2,1)S(1)} %get-tuple-element.66), dimensions={0,2} | broadcast | bytes 2097184 | tf_op jit(solution)/shard_map/mul | solution.py:74
  4.4 6.0 %mul.16 = bf16[64,16384]{1,0:T(8,128)(2,1)} reshape(bf16[2,32,8,32,64]{4,3,2,1,0:T(8,128)(2,1)} %mul.15) | data formatting | bytes 4194304 | tf_op jit(solution)/shard_map/mul | solution.py:74
  10.4 2.7 %mul.17 = bf16[64,16384]{1,0:T(8,128)(2,1)S(1)} multiply(bf16[64,16384]{1,0:T(8,128)(2,1)} %param.6, bf16[64,16384]{1,0:T(8,128)(2,1)} %mul.16) | non-fusion elementwise | flops 1048576 | bytes 6291456 | tf_op jit(solution)/shard_map/mul | solution.py:74
  13.2 1.9 %collective-permute-start = (bf16[1,16384]{1,0:T(2,128)(2,1)S(1)}, bf16[1,16384]{1,0:T(2,128)(2,1)S(1)}, u32[]{:S(2)}, u32[]{:S(2)}) collective-permute-start(bf16[1,16384]{1,0:T(2,128)(2,1)S(1)} %get-tuple-element.60), channel_id=1, source_target_pairs={{0,1},{1,2},{2,3},{3,4},{4,5},{5,6},{6,7},{7,8},{8,9},{9,10},{10,1... | collective-permute-start | bytes 98312 | tf_op jit(solution)/shard_map/ppermute | solution.py:17
  15.1 3.6 %collective-permute-start.1 = (bf16[1,16384]{1,0:T(2,128)(2,1)S(1)}, bf16[1,16384]{1,0:T(2,128)(2,1)S(1)}, u32[]{:S(2)}, u32[]{:S(2)}) collective-permute-start(bf16[1,16384]{1,0:T(2,128)(2,1)S(1)} %get-tuple-element.61), channel_id=1, source_target_pairs={{1,0},{2,1},{3,2},{4,3},{5,4},{6,5},{7,6},{8,7},{9,8},{10,9},{11,1... | collective-permute-start | bytes 98312 | tf_op jit(solution)/shard_map/ppermute | solution.py:18
  19.4 1.4 %dynamic-update-slice = s32[16]{0:T(128)S(1)} dynamic-update-slice(s32[16]{0:T(128)S(1)} %broadcast.389, s32[1]{0:T(128)} %bitcast.1, u32[]{:T(128)} %bitcast.2) | dynamic-update-slice | bytes 12
  20.8 8.2 %all-reduce.2 = s32[16]{0:T(128)S(1)} all-reduce(s32[16]{0:T(128)S(1)} %dynamic-update-slice), channel_id=1, replica_groups=mesh['slides'=2,'row'=16] {'row'}, use_global_device_ids=true, to_apply=%add.2 | all-reduce | flops 16 | bytes 128
  29.0 17.3 %while.10 = (s32[]{:T(128)}, s32[1]{0:T(128)}, s32[]{:T(128)}, s32[16,1]{0,1:T(1,128)S(1)}, s32[]{:T(128)}, /*index=5*/s32[]{:T(128)}, s32[]{:T(128)}) while((s32[]{:T(128)}, s32[1]{0:T(128)}, s32[]{:T(128)}, s32[16,1]{0,1:T(1,128)S(1)}, s32[]{:T(128)}, /*index=5*/s32[]{:T(128)}, s32[]{:T(128)}) %tuple.44), condition=%wide.region_2.3_spmd, body=%wide.region_1.2_spmd.sunk | while | flops 6 | bytes 143 | solution.py:31
  34.0 0.6 constant_dynamic-slice_fusion.2
  35.2 0.6 constant_dynamic-slice_fusion.2
  36.4 0.6 constant_dynamic-slice_fusion.2
  37.7 0.6 constant_dynamic-slice_fusion.2
  46.4 1.3 %sort.17 = (s32[16]{0:T(128)}, s32[16]{0:T(128)S(1)}) sort(s32[16]{0:T(128)S(1)} %sub.67, s32[16]{0:T(128)S(1)} %iota.23), dimensions={0}, to_apply=%region_3.4 | sort | flops 64 | bytes 256 | tf_op jit(solution)/shard_map/jit(argsort)/sort | solution.py:89
  47.7 0.6 gather_fusion
  48.4 0.7 compare_and_fusion.2
  49.1 0.6 gather_fusion.2
  49.7 0.7 compare_and_fusion
  50.4 5.7 %concatenate.30 = bf16[64,256,64]{2,1,0:T(8,128)(2,1)} reshape(bf16[64,16384]{1,0:T(8,128)(2,1)S(1)} %mul.17) | data formatting | bytes 4194304 | tf_op jit(solution)/shard_map/concatenate | solution.py:19
  56.7 4.5 %constant_dynamic-update-slice_fusion.3 = (bf16[65,256,64]{2,1,0:T(8,128)(2,1)S(1)}, bf16[65,256,64]{2,1,0:T(8,128)(2,1)S(1)}) fusion(bf16[64,256,64]{2,1,0:T(8,128)(2,1)} %concatenate.30, bf16[65,256,64]{2,1,0:T(8,128)(2,1)S(1)} %constant_dynamic-update-slice_fusion.1), kind=kLoop, calls=%fused_computation.20 | loop fusion | bytes 10485760
  61.3 6.4 %fusion.5 = bf16[66,258,64]{2,1,0:T(8,128)(2,1)} fusion(bf16[1,256,64]{2,1,0:T(8,128)(2,1)S(1)} %concatenate.31, bf16[64,256,64]{2,1,0:T(8,128)(2,1)S(1)} %copy-done, bf16[1,256,64]{2,1,0:T(8,128)(2,1)S(1)} %concatenate.29), kind=kLoop, calls=%fused_computation.12 | loop fusion | flops 13077504 | bytes 4342272 | tf_op jit(solution)/shard_map/concatenate | solution.py:19
  67.7 1.0 fusion.13
  69.0 1.6 %fusion.12 = (bf16[34,34,64]{2,1,0:T(8,128)(2,1)S(1)}, bf16[34,34,64]{2,1,0:T(8,128)(2,1)S(1)}, bf16[34,34,64]{2,1,0:T(8,128)(2,1)S(1)}, bf16[34,34,64]{2,1,0:T(8,128)(2,1)S(1)}) fusion(bf16[66,258,64]{2,1,0:T(8,128)(2,1)} %fusion.5), kind=kLoop, calls=%fused_computation.66 | loop fusion | bytes 1183744 | tf_op jit(solution)/shard_map/slice | solution.py:81
  70.8 0.9 stack_reshape.56
  71.7 0.9 stack_reshape.55
  72.6 0.9 stack_reshape.48
  73.6 0.9 stack_reshape.61
  74.4 0.9 stack_reshape.60
  75.4 0.9 stack_reshape.59
  76.3 0.9 stack_reshape.58
  77.2 0.9 stack_reshape.57
  78.1 2.7 %fusion.14 = (bf16[34,34,64]{2,1,0:T(8,128)(2,1)S(1)}, bf16[34,34,64]{2,1,0:T(8,128)(2,1)S(1)}, bf16[34,34,64]{2,1,0:T(8,128)(2,1)S(1)}, bf16[34,34,64]{2,1,0:T(...) fusion(bf16[65,256,64]{2,1,0:T(8,128)(2,1)} %copy-done.2), kind=kLoop, calls=%fused_computation.68 | loop fusion | bytes 1775616 | tf_op jit(solution)/shard_map/slice | solution.py:81
  80.8 0.9 stack_reshape.54
  81.7 0.9 stack_reshape.53
  82.6 0.9 stack_reshape.52
  83.5 0.9 stack_reshape.51
  84.5 0.9 stack_reshape.50
  85.4 0.9 stack_reshape.49
  86.3 0.9 constant_dynamic-update-slice_fusion.19
  87.2 0.9 constant_dynamic-update-slice_fusion.18
  88.2 0.9 constant_dynamic-update-slice_fusion.17
  89.1 0.9 constant_dynamic-update-slice_fusion.16
  90.1 0.9 constant_dynamic-update-slice_fusion.15
  91.0 0.9 constant_dynamic-update-slice_fusion.14
  91.9 0.9 constant_dynamic-update-slice_fusion.13
  92.9 0.9 constant_dynamic-update-slice_fusion.12
  93.8 0.9 constant_dynamic-update-slice_fusion.11
  94.7 0.9 constant_dynamic-update-slice_fusion.10
  95.7 0.9 constant_dynamic-update-slice_fusion.9
  96.6 0.9 constant_dynamic-update-slice_fusion.8
  97.6 0.9 constant_dynamic-update-slice_fusion.7
  98.5 0.9 constant_dynamic-update-slice_fusion.6
  99.5 0.6 gather_fusion.3
  100.2 2.1 %collective-permute-start.2 = (bf16[2,34,2176]{2,1,0:T(8,128)(2,1)S(1)}, bf16[2,34,2176]{2,1,0:T(8,128)(2,1)}, u32[]{:S(2)}, u32[]{:S(2)}) collective-permute-start(bf16[2,34,2176]{2,1,0:T(8,128)(2,1)S(1)} %select_select_fusion), channel_id=1, source_target_pairs={{0,1},{1,2},{2,3},{3,4},{4,5},{5,6},{6,7},{7,8},{8,9},{9,10},{10,1... | collective-permute-start | bytes 887816 | tf_op jit(solution)/shard_map/ppermute | solution.py:37
  102.4 1.5 %fusion.17 = (bf16[1,3,64,64]{3,2,1,0:T(8,128)(2,1)S(1)}, bf16[1,3,64,64]{3,2,1,0:T(8,128)(2,1)}, bf16[1,3,64,64]{3,2,1,0:T(8,128)(2,1)}) fusion(bf16[3,3,64,64]{3,2,1,0:T(8,128)(2,1)} %param.8), kind=kLoop, calls=%fused_computation.71 | loop fusion | bytes 147456 | tf_op jit(solution)/shard_map/slice | solution.py:54
  103.9 2.5 %gather_fusion.1 = bf16[8,34,2176]{2,1,0:T(8,128)(2,1)S(1)} fusion(bf16[16,34,2176]{2,1,0:T(8,128)(2,1)} %copy-done.1, s32[1024]{0:T(1024)S(1)} %pad_clamp_fusion.2), kind=kCustom, calls=%fused_computation.1 | custom fusion | bytes 2367520 | tf_op jit(solution)/shard_map/jit(_take)/gather | solution.py:97
  106.5 2.5 %collective-permute-done.2 = bf16[2,34,2176]{2,1,0:T(8,128)(2,1)} collective-permute-done((bf16[2,34,2176]{2,1,0:T(8,128)(2,1)S(1)}, bf16[2,34,2176]{2,1,0:T(8,128)(2,1)}, u32[]{:S(2)}, u32[]{:S(2)}) %collective-permute-start.2) | collective-permute-done | bytes 295968 | tf_op jit(solution)/shard_map/ppermute | solution.py:37
  109.0 2.4 %pad_add_fusion = bf16[8,34,2176]{2,1,0:T(8,128)(2,1)} fusion(bf16[2,34,2176]{2,1,0:T(8,128)(2,1)} %collective-permute-done.2, bf16[8,34,2176]{2,1,0:T(8,128)(2,1)S(1)} %gather_fusion.1, pred[8]{0:T(512)(128)(4,1)S(1)} %get-tuple-element.70, pred[8]{0:T(512)(128)(4,1)S(1)} %get-tuple-element.71), kind=kLoop, calls=%fused_computation.15 | loop fusion | flops 1775616 | bytes 2663440 | tf_op jit(solution)/shard_map/add | solution.py:108
  111.3 3.3 %reshape.195 = bf16[8,34,34,64]{3,2,1,0:T(8,128)(2,1)S(1)} reshape(bf16[8,34,2176]{2,1,0:T(8,128)(2,1)} %pad_add_fusion) | data formatting | bytes 2367488 | tf_op jit(solution)/shard_map/reshape | solution.py:48
  114.7 1.6 %fusion.15 = (bf16[8,34,32,64]{3,2,1,0:T(8,128)(2,1)S(1)}, bf16[8,34,32,64]{3,2,1,0:T(8,128)(2,1)S(1)}, bf16[8,34,32,64]{3,2,1,0:T(8,128)(2,1)S(1)}) fusion(bf16[8,34,34,64]{3,2,1,0:T(8,128)(2,1)S(1)} %reshape.195), kind=kLoop, calls=%fused_computation.69 | loop fusion | bytes 6684672 | tf_op jit(solution)/shard_map/slice | solution.py:50
  116.3 2.4 %fusion.10 = f32[8,32,32,64]{3,2,1,0:T(8,128)S(1)} fusion(bf16[192,64,1,1]{1,0,3,2:T(8,128)(2,1)S(1)} %bitcast.41, bf16[8,34,32,64]{3,2,1,0:T(8,128)(2,1)S(1)} %get-tuple-element.59, bf16[8,34,32,64]{3,2,1,0:T(8,128)(2,1)S(1)} %get-tuple-element.58, bf16[8,34,32,64]{3,2,1,0:T(8,128)(2,1)S(1)} %get-tuple-element.57), kind=kOutput, calls=%fused_computation.64 | convolution fusion | flops 211353600 | bytes 5464064 | tf_op jit(solution)/shard_map/nhwk,ko->nhwo/dot_general | solution.py:55
  118.7 2.3 %fusion.11 = f32[8,32,32,64]{3,2,1,0:T(8,128)S(1)} fusion(bf16[192,64,1,1]{1,0,3,2:T(8,128)(2,1)S(1)} %bitcast.40, bf16[8,34,32,64]{3,2,1,0:T(8,128)(2,1)S(1)} %get-tuple-element.59, bf16[8,34,32,64]{3,2,1,0:T(8,128)(2,1)S(1)} %get-tuple-element.58, bf16[8,34,32,64]{3,2,1,0:T(8,128)(2,1)S(1)} %get-tuple-element.57), kind=kOutput, calls=%fused_computation.65 | convolution fusion | flops 211353600 | bytes 5464064 | tf_op jit(solution)/shard_map/nhwk,ko->nhwo/dot_general | solution.py:55
  121.1 2.8 %add_convert_fusion = bf16[8,32,32,64]{3,2,1,0:T(8,128)(2,1)S(1)} fusion(f32[8,32,32,64]{3,2,1,0:T(8,128)S(1)} %fusion.11, f32[8,32,32,64]{3,2,1,0:T(8,128)S(1)} %fusion.10, bf16[192,64,1,1]{1,0,3,2:T(8,128)(2,1)S(1)} %bitcast.39, f32[64]{0:T(128)S(1)} %convert_element_type.14, bf16[8,34,32,64]{3,2,1,0:T(8,128)(2,1)S(1)} %get-tuple-element.59, ...), kind=kOutput, calls=%fused_computation.14 | convolution fusion | flops 213450752 | bytes 8610048 | tf_op jit(solution)/shard_map/nhwk,ko->nhwo/dot_general | solution.py:55
  123.9 2.4 %reshape.153 = bf16[8,32,2048]{2,1,0:T(8,128)(2,1)} reshape(bf16[8,32,32,64]{3,2,1,0:T(8,128)(2,1)S(1)} %add_convert_fusion) | data formatting | bytes 2097152 | tf_op jit(solution)/shard_map/reshape | solution.py:62
  (51 shorter events, 8.0 us)
Async XLA Ops:
  10.4 8.4 %copy-start.6 = (u32[32]{0:T(128)S(1)}, u32[32]{0:T(128)}, u32[]{:S(2)}) copy-start(u32[32]{0:T(128)} %constant.86) | copy-start | bytes 388
  13.2 42.9 %collective-permute-start = (bf16[1,16384]{1,0:T(2,128)(2,1)S(1)}, bf16[1,16384]{1,0:T(2,128)(2,1)S(1)}, u32[]{:S(2)}, u32[]{:S(2)}) collective-permute-start(bf16[1,16384]{1,0:T(2,128)(2,1)S(1)} %get-tuple-element.60), channel_id=1, source_target_pairs={{0,1},{1,2},{2,3},{3,4},{4,5},{5,6},{6,7},{7,8},{8,9},{9,10},{10,1... | collective-permute-start | bytes 98312 | tf_op jit(solution)/shard_map/ppermute | solution.py:17
  15.1 41.3 %collective-permute-start.1 = (bf16[1,16384]{1,0:T(2,128)(2,1)S(1)}, bf16[1,16384]{1,0:T(2,128)(2,1)S(1)}, u32[]{:S(2)}, u32[]{:S(2)}) collective-permute-start(bf16[1,16384]{1,0:T(2,128)(2,1)S(1)} %get-tuple-element.61), channel_id=1, source_target_pairs={{1,0},{2,1},{3,2},{4,3},{5,4},{6,5},{7,6},{8,7},{9,8},{10,9},{11,1... | collective-permute-start | bytes 98312 | tf_op jit(solution)/shard_map/ppermute | solution.py:18
  50.4 5.7 %copy-start.5 = (bf16[64]{0:T(256)(128)(2,1)S(1)}, bf16[64]{0:T(256)(128)(2,1)}, u32[]{:S(2)}) copy-start(bf16[64]{0:T(256)(128)(2,1)} %param.9) | copy-start | bytes 388
  56.7 4.5 %copy-start = (bf16[64,256,64]{2,1,0:T(8,128)(2,1)S(1)}, bf16[64,256,64]{2,1,0:T(8,128)(2,1)}, u32[]{:S(2)}) copy-start(bf16[64,256,64]{2,1,0:T(8,128)(2,1)} %concatenate.30) | copy-start | bytes 6291460
  61.3 6.5 %copy-start.2 = (bf16[65,256,64]{2,1,0:T(8,128)(2,1)}, bf16[65,256,64]{2,1,0:T(8,128)(2,1)S(1)}, u32[]{:S(2)}) copy-start(bf16[65,256,64]{2,1,0:T(8,128)(2,1)S(1)} %get-tuple-element.56) | copy-start | bytes 6389764
  99.5 2.9 %copy-start.1 = (bf16[16,34,2176]{2,1,0:T(8,128)(2,1)}, bf16[16,34,2176]{2,1,0:T(8,128)(2,1)S(1)}, u32[]{:S(2)}) copy-start(bf16[16,34,2176]{2,1,0:T(8,128)(2,1)S(1)} %constant_dynamic-update-slice_fusion.4) | copy-start | bytes 7102468
  100.2 8.7 %collective-permute-start.2 = (bf16[2,34,2176]{2,1,0:T(8,128)(2,1)S(1)}, bf16[2,34,2176]{2,1,0:T(8,128)(2,1)}, u32[]{:S(2)}, u32[]{:S(2)}) collective-permute-start(bf16[2,34,2176]{2,1,0:T(8,128)(2,1)S(1)} %select_select_fusion), channel_id=1, source_target_pairs={{0,1},{1,2},{2,3},{3,4},{4,5},{5,6},{6,7},{7,8},{8,9},{9,10},{10,1... | collective-permute-start | bytes 887816 | tf_op jit(solution)/shard_map/ppermute | solution.py:37
  114.7 1.6 %copy-start.4 = (bf16[1,3,64,64]{3,2,1,0:T(8,128)(2,1)S(1)}, bf16[1,3,64,64]{3,2,1,0:T(8,128)(2,1)}, u32[]{:S(2)}) copy-start(bf16[1,3,64,64]{3,2,1,0:T(8,128)(2,1)} %get-tuple-element.64) | copy-start | bytes 73732
  116.3 2.4 %copy-start.3 = (bf16[1,3,64,64]{3,2,1,0:T(8,128)(2,1)S(1)}, bf16[1,3,64,64]{3,2,1,0:T(8,128)(2,1)}, u32[]{:S(2)}) copy-start(bf16[1,3,64,64]{3,2,1,0:T(8,128)(2,1)} %get-tuple-element.63) | copy-start | bytes 73732
where the time goes:
time: 127 us; the launch traced here: 126 us
  local copies, waits for them, and re-layouts  74.9 us (59%)
  other arithmetic  16.1 us (13%)
  loops' own time  9 us (7%)
  blocking collectives  8.24 us (6%)
  starting transfers between devices  7.7 us (6%)
  matrix products  7.52 us (6%)
  waiting for transfers between devices  2.5 us (2%)
    unnamed x34, local copies, waits for them, and re-layouts  19.7 us
    another operation x17, local copies, waits for them, and re-layouts, on_device(): padded_tiles = jnp.stack(pieces)  13.3 us
    another operation x1, loops' own time, entering(): return lax.fori_loop(0, place, one, state)  9 us
    mul x2, local copies, waits for them, and re-layouts, on_device(): blocks * keeps  8.98 us
    dynamic_slice x14, local copies, waits for them, and re-layouts, one(): return combine(state, lax.dynamic_index_in_dim(gathered, step, 0, False))  8.32 us
    unnamed x1, blocking collectives  8.24 us
    dot_general x3, matrix products, convolve(): jnp.einsum('nhwk,ko->nhwo', widened[:, vertical:vertical + side], kernel,...  7.52 us
    concatenate x1, other arithmetic, extended(): array = jnp.concatenate([before, array, after], axis=dim)  6.44 us
  transfers between devices with their start and end apart: 3, of which 1 were waited for; matrix products, arithmetic and copies ran while one was open for 19% of the time, Pallas kernels for 0%

commit v1 on v0

v1 whole, which is shorter than its diff:
```python
import functools

import jax
import jax.numpy as jnp
from jax import lax
from jax.experimental import pallas as pl
from jax.experimental.pallas import tpu as pltpu
from jax.sharding import PartitionSpec as P

SLOTS = 8
SHIFT_MOST = 2
LANES = 128
PACK = 16
MESH = pl.DeviceIdType.MESH


def kernel(
    n, side, channels,
    x_ref, mask_s, mask_v, w_ref, b_ref, out_ref,
    image, conv, low, rows3, wide, masks, stage_up, stage_dn, halo_top, halo_bot, onward, arrived,
    x_sem, mask_send, mask_recv, halo_send, halo_recv, tile_send, tile_recv,
):
    band_rows, cols = mask_s.shape
    height = band_rows * side
    width = side * channels
    tiles = band_rows * cols
    quad = 2 * LANES
    groups = width // quad
    per = quad // channels
    half = LANES // channels
    me = lax.axis_index("row")

    def fetch(c):
        return pltpu.make_async_copy(
            x_ref.at[:, pl.ds(c * width, width)],
            image.at[pl.ds(PACK, height), pl.ds(LANES + c * width, width)],
            x_sem.at[c],
        )

    for c in range(cols):
        fetch(c).start()

    barrier = pltpu.get_barrier_semaphore()

    def greet(j, carry):
        pl.semaphore_signal(
            barrier, inc=1, device_id={"row": lax.rem(me + j, n)}, device_id_type=MESH
        )
        return carry

    lax.fori_loop(1, n, greet, 0)

    none = jnp.zeros((channels, channels), jnp.bfloat16)
    for dy in range(3):
        taps = [w_ref[dy, 0], w_ref[dy, 1], w_ref[dy, 2]]
        for p in range(2 * per):
            for q in range(per // half):
                u = p - half - half * q
                parts = [taps[u + 1 - o] if 0 <= u + 1 - o <= 2 else none for o in range(half)]
                wide[dy, p * channels:(p + 1) * channels, q * LANES:(q + 1) * LANES] = (
                    jnp.concatenate(parts, axis=1)
                )
    edge = jnp.zeros((height + 2 * PACK, LANES), jnp.bfloat16)
    image[:, 0:LANES] = edge
    image[:, LANES + cols * width:2 * LANES + cols * width] = edge
    masks[me] = mask_v[...]
    blank_rows = jnp.zeros((PACK, cols * width), jnp.bfloat16)
    image[0:PACK, LANES:LANES + cols * width] = blank_rows
    image[PACK + height:2 * PACK + height, LANES:LANES + cols * width] = blank_rows

    firsts, lasts = [], []
    for c in range(cols):
        fetch(c).wait()
        for r in range(band_rows):
            keep = jnp.full((side, LANES), mask_s[r, c], jnp.int32).astype(jnp.float32)
            keep = keep.astype(jnp.bfloat16)
            for k in range(width // LANES):
                at = (pl.ds(PACK + r * side, side), pl.ds(LANES + c * width + k * LANES, LANES))
                image[at] = image[at] * keep
        span = pl.ds(LANES + c * width, width)
        first = image[PACK:2 * PACK, span].astype(jnp.float32)
        last = image[height:height + PACK, span].astype(jnp.float32)
        firsts.append(first[0:1])
        lasts.append(last[PACK - 1:PACK])
    stage_up[...] = jnp.concatenate(firsts, axis=0).astype(jnp.bfloat16)
    stage_dn[...] = jnp.concatenate(lasts, axis=0).astype(jnp.bfloat16)

    pl.semaphore_wait(barrier, n - 1)

    down = pltpu.make_async_remote_copy(
        stage_dn, halo_top, halo_send.at[0], halo_recv.at[0],
        device_id={"row": lax.rem(me + 1, n)}, device_id_type=MESH)
    up = pltpu.make_async_remote_copy(
        stage_up, halo_bot, halo_send.at[1], halo_recv.at[1],
        device_id={"row": lax.rem(me + n - 1, n)}, device_id_type=MESH)
    is_first = me == 0
    is_last = me == n - 1

    @pl.when(jnp.logical_not(is_last))
    def _():
        down.start()

    @pl.when(jnp.logical_not(is_first))
    def _():
        up.start()

    def mask_copy(target, slot):
        return pltpu.make_async_remote_copy(
            mask_v, masks.at[slot], mask_send.at[target], mask_recv.at[slot],
            device_id={"row": target}, device_id_type=MESH)

    def tell(j, carry):
        mask_copy(lax.rem(me + j, n), me).start()
        return carry

    lax.fori_loop(1, n, tell, 0)

    bias = b_ref[...].astype(jnp.float32)
    bias = jnp.concatenate([bias] * per, axis=1)
    duo = 2
    duos = cols // duo
    bands = duo * groups

    def convolve(r, pair, carry):
        left = pl.multiple_of(pair * (duo * width), duo * width)
        for k in range(bands + 1):
            block = image[r * side:(r + 1) * side + 2 * PACK, pl.ds(left + k * quad, quad)]
            span = pl.ds(k * quad, quad)
            block32 = block.astype(jnp.float32)
            rows3[0, :, span] = block32[PACK - 1:PACK - 1 + side].astype(jnp.bfloat16)
            rows3[1, :, span] = block[PACK:PACK + side]
            rows3[2, :, span] = block32[PACK + 1:PACK + 1 + side].astype(jnp.bfloat16)
        total = jnp.broadcast_to(bias, (bands * side, quad))
        for dy in range(3):
            left_side = jnp.concatenate(
                [rows3[dy, :, g * quad:(g + 2) * quad] for g in range(bands)], axis=0)
            total = total + jnp.dot(
                left_side, wide[dy], preferred_element_type=jnp.float32)
        done = total.astype(jnp.bfloat16)
        for g in range(bands):
            at = g % groups * quad
            tile_at = r * cols + pair * duo + g // groups
            conv[tile_at, :, at:at + quad] = done[g * side:(g + 1) * side]
            if r == band_rows - 1:
                low[pair * duo + g // groups, :, at:at + quad] = (
                    total[(g + 1) * side - 8:(g + 1) * side])
        return carry

    lax.fori_loop(0, duos, functools.partial(convolve, band_rows - 1), 0)

    @pl.when(jnp.logical_not(is_first))
    def _():
        down.wait_recv()
        lines = halo_top[...].astype(jnp.float32)
        for c in range(cols):
            image[0:PACK, LANES + c * width:LANES + (c + 1) * width] = (
                jnp.broadcast_to(lines[c:c + 1], (PACK, width)).astype(jnp.bfloat16))

    for r in range(band_rows - 2, 0, -1):
        lax.fori_loop(0, duos, functools.partial(convolve, r), 0)
    lax.fori_loop(duos - 1, duos, functools.partial(convolve, 0), 0)

    @pl.when(jnp.logical_not(is_last))
    def _():
        up.wait_recv()
        lines = halo_bot[...].astype(jnp.float32)
        blank = jnp.zeros((1, LANES), jnp.float32)
        before = jnp.concatenate([blank, lines[0:cols - 1, width - LANES:width]], axis=0)
        after = jnp.concatenate([lines[1:cols, 0:LANES], blank], axis=0)
        lines = jnp.concatenate([before, lines, after], axis=1)
        stack = jnp.concatenate(
            [lines[:, g * quad:(g + 2) * quad] for g in range(groups)], axis=0)
        more = jnp.dot(
            stack.astype(jnp.bfloat16), wide[2], preferred_element_type=jnp.float32)
        lowest = lax.broadcasted_iota(jnp.int32, (PACK, quad), 0) == PACK - 1
        for c in range(cols):
            for g in range(groups):
                at = g * quad
                row = low[c, 7:8, at:at + quad] + more[g * cols + c:g * cols + c + 1]
                where = ((band_rows - 1) * cols + c, pl.ds(side - PACK, PACK), pl.ds(at, quad))
                old = conv[where].astype(jnp.float32)
                new = jnp.where(lowest, jnp.broadcast_to(row, (PACK, quad)), old)
                conv[where] = new.astype(jnp.bfloat16)

    def told(j, carry):
        mask_copy(lax.rem(me + j, n), lax.rem(me + j, n)).wait_recv()
        return carry

    lax.fori_loop(1, n, told, 0)
    device = lax.broadcasted_iota(jnp.int32, masks.shape, 0)
    excess = jnp.sum(jnp.where(device < me, masks[...], 0)) - SLOTS * me
    seen = []
    for r in range(band_rows):
        for c in range(cols):
            seen.append(mask_s[r, c] + (seen[-1] if seen else 0))

    def place(rank):
        total = jnp.int32(0)
        for count in seen:
            total = total + jnp.where(count <= rank, 1, 0)
        return jnp.minimum(total, tiles - 1)

    for k in range(SHIFT_MOST):
        onward[k] = conv[place(SLOTS + k - excess)]
    tile = pltpu.make_async_remote_copy(
        onward, arrived, tile_send, tile_recv,
        device_id={"row": lax.rem(me + 1, n)}, device_id_type=MESH)

    @pl.when(jnp.logical_not(is_last))
    def _():
        tile.start()

    lax.fori_loop(0, duos - 1, functools.partial(convolve, 0), 0)

    for k in range(SLOTS):
        out_ref[k] = conv[place(k - excess)]

    @pl.when(jnp.logical_not(is_first))
    def _():
        tile.wait_recv()
        for k in range(SHIFT_MOST):
            own = out_ref[k].astype(jnp.float32)
            theirs = arrived[k].astype(jnp.float32)
            late = jnp.full(own.shape, excess, jnp.int32) > k
            out_ref[k] = jnp.where(late, theirs, own).astype(jnp.bfloat16)
        up.wait_send()

    @pl.when(jnp.logical_not(is_last))
    def _():
        down.wait_send()
        tile.wait_send()

    def sent(j, carry):
        mask_copy(lax.rem(me + j, n), me).wait_send()
        return carry

    lax.fori_loop(1, n, sent, 0)


def on_device(slide_pixels, tissue_mask, conv_weight, conv_bias):
    n = lax.axis_size("row")
    band_rows, cols = tissue_mask.shape
    channels = conv_weight.shape[2]
    height = slide_pixels.shape[0]
    side = height // band_rows
    width = side * channels
    quad = 2 * LANES
    vmem = pl.BlockSpec(memory_space=pltpu.VMEM)
    bf16 = jnp.bfloat16
    return pl.pallas_call(
        functools.partial(kernel, n, side, channels),
        out_shape=jax.ShapeDtypeStruct((SLOTS, side, width), bf16),
        in_specs=[
            pl.BlockSpec(memory_space=pl.ANY),
            pl.BlockSpec(memory_space=pltpu.SMEM),
            vmem, vmem, vmem,
        ],
        out_specs=vmem,
        scratch_shapes=[
            pltpu.VMEM((height + 2 * PACK, cols * width + 2 * LANES), bf16),
            pltpu.VMEM((band_rows * cols, side, width), bf16),
            pltpu.VMEM((cols, 8, width), jnp.float32),
            pltpu.VMEM((3, side, 2 * width + quad), bf16),
            pltpu.VMEM((3, 2 * quad, quad), bf16),
            pltpu.VMEM((n, band_rows, cols), jnp.int32),
            pltpu.VMEM((cols, width), bf16),
            pltpu.VMEM((cols, width), bf16),
            pltpu.VMEM((cols, width), bf16),
            pltpu.VMEM((cols, width), bf16),
            pltpu.VMEM((SHIFT_MOST, side, width), bf16),
            pltpu.VMEM((SHIFT_MOST, side, width), bf16),
            pltpu.SemaphoreType.DMA((cols,)),
            pltpu.SemaphoreType.DMA((n,)),
            pltpu.SemaphoreType.DMA((n,)),
            pltpu.SemaphoreType.DMA((2,)),
            pltpu.SemaphoreType.DMA((2,)),
            pltpu.SemaphoreType.DMA,
            pltpu.SemaphoreType.DMA,
        ],
        compiler_params=pltpu.CompilerParams(collective_id=0, has_side_effects=True),
    )(slide_pixels, tissue_mask, tissue_mask, conv_weight, conv_bias.reshape(1, channels))


def solution(mesh):
    return jax.shard_map(
        on_device,
        mesh=mesh,
        in_specs=(P(("slides", "row"), None), P(("slides", "row"), None), P(), P()),
        out_specs=P(("slides", "row"), None, None),
        check_vma=False,
    )
```

time: 127 us -> 17.9 us (0.14)
  the two profiles are of different devices: /device:TPU:26 before, /device:TPU:8 now
where the time goes in v1:
time: 17.9 us; the launch traced here: 17.7 us
  Pallas kernels  15.3 us (85%)
  local copies, waits for them, and re-layouts  2.3 us (13%)
    pallas_call x1, Pallas kernels, on_device(): pl.pallas_call(functools.partial(kernel, n, side, channels), out_shape=ja...  15.3 us
    unnamed x1, local copies, waits for them, and re-layouts  2.3 us

profile of v1, /device:TPU:8, one launch (start us, length us, event | category | flops | bytes accessed | tf_op | source)
XLA Modules:
  0.0 17.7 jit_solution(6387880659645760308)
XLA Ops:
  0.0 15.3 %shard_map.46 = bf16[8,32,2048]{2,1,0:T(8,128)(2,1)} custom-call(bf16[64,16384]{1,0:T(8,128)(2,1)} %x_ref.1, s32[2,8]{1,0:T(2,128)} %mask_v.1, s32[2,8]{1,0:T(2,128)} %mask_v.1, bf16[3,3,64,64]{3,2,1,0:T(8,128)(2,1)} %w_ref.1, bf16[1,64]{1,0:T(2,128)(2,1)} %bitcast.1), custom_call_target="tpu_custom_call" | custom-call | tf_op jit(solution)/shard_map/pallas_call | solution.py:250
  15.4 2.3 %copy.6 = bf16[8,32,2048]{2,1,0:T(8,128)(2,1)} copy(bf16[8,32,2048]{2,1,0:T(8,128)(2,1)} %shard_map.46) | data formatting | bytes 2097152

commit v2 on v1

--- a/solution.py
+++ b/solution.py
@@ -16,9 +16,10 @@
 
 def kernel(
     n, side, channels,
-    x_ref, mask_s, mask_v, w_ref, b_ref, out_ref,
+    x_ref, mask_s, mask_v, w_ref, b_ref, out_any,
     image, conv, low, rows3, wide, masks, stage_up, stage_dn, halo_top, halo_bot, onward, arrived,
     x_sem, mask_send, mask_recv, halo_send, halo_recv, tile_send, tile_recv,
+    out_ref, out_sem,
 ):
     band_rows, cols = mask_s.shape
     height = band_rows * side
@@ -30,6 +31,16 @@
     half = LANES // channels
     me = lax.axis_index("row")
 
+    barrier = pltpu.get_barrier_semaphore()
+
+    def greet(j, carry):
+        pl.semaphore_signal(
+            barrier, inc=1, device_id={"row": lax.rem(me + j, n)}, device_id_type=MESH
+        )
+        return carry
+
+    lax.fori_loop(1, n, greet, 0)
+
     def fetch(c):
         return pltpu.make_async_copy(
             x_ref.at[:, pl.ds(c * width, width)],
@@ -39,16 +50,6 @@
 
     for c in range(cols):
         fetch(c).start()
-
-    barrier = pltpu.get_barrier_semaphore()
-
-    def greet(j, carry):
-        pl.semaphore_signal(
-            barrier, inc=1, device_id={"row": lax.rem(me + j, n)}, device_id_type=MESH
-        )
-        return carry
-
-    lax.fori_loop(1, n, greet, 0)
 
     none = jnp.zeros((channels, channels), jnp.bfloat16)
     for dy in range(3):
@@ -130,12 +131,11 @@
             rows3[0, :, span] = block32[PACK - 1:PACK - 1 + side].astype(jnp.bfloat16)
             rows3[1, :, span] = block[PACK:PACK + side]
             rows3[2, :, span] = block32[PACK + 1:PACK + 1 + side].astype(jnp.bfloat16)
-        total = jnp.broadcast_to(bias, (bands * side, quad))
-        for dy in range(3):
-            left_side = jnp.concatenate(
-                [rows3[dy, :, g * quad:(g + 2) * quad] for g in range(bands)], axis=0)
-            total = total + jnp.dot(
-                left_side, wide[dy], preferred_element_type=jnp.float32)
+        left_side = jnp.concatenate([jnp.concatenate(
+            [rows3[dy, :, g * quad:(g + 2) * quad] for g in range(bands)], axis=0)
+            for dy in range(3)], axis=1)
+        total = jnp.dot(left_side, wide[...].reshape(6 * quad, quad),
+            preferred_element_type=jnp.float32) + bias
         done = total.astype(jnp.bfloat16)
         for g in range(bands):
             at = g % groups * quad
@@ -182,13 +182,6 @@
                 new = jnp.where(lowest, jnp.broadcast_to(row, (PACK, quad)), old)
                 conv[where] = new.astype(jnp.bfloat16)
 
-    def told(j, carry):
-        mask_copy(lax.rem(me + j, n), lax.rem(me + j, n)).wait_recv()
-        return carry
-
-    lax.fori_loop(1, n, told, 0)
-    device = lax.broadcasted_iota(jnp.int32, masks.shape, 0)
-    excess = jnp.sum(jnp.where(device < me, masks[...], 0)) - SLOTS * me
     seen = []
     for r in range(band_rows):
         for c in range(cols):
@@ -201,7 +194,7 @@
         return jnp.minimum(total, tiles - 1)
 
     for k in range(SHIFT_MOST):
-        onward[k] = conv[place(SLOTS + k - excess)]
+        onward[k] = conv[place(seen[-1] - SHIFT_MOST + k)]
     tile = pltpu.make_async_remote_copy(
         onward, arrived, tile_send, tile_recv,
         device_id={"row": lax.rem(me + 1, n)}, device_id_type=MESH)
@@ -212,19 +205,40 @@
 
     lax.fori_loop(0, duos - 1, functools.partial(convolve, 0), 0)
 
-    for k in range(SLOTS):
+    def told(j, carry):
+        mask_copy(lax.rem(me + j, n), lax.rem(me + j, n)).wait_recv()
+        return carry
+
+    lax.fori_loop(1, n, told, 0)
+    device = lax.broadcasted_iota(jnp.int32, masks.shape, 0)
+    excess = jnp.sum(jnp.where(device < me, masks[...], 0)) - SLOTS * me
+
+    def give(k):
+        return pltpu.make_async_copy(out_ref.at[k], out_any.at[k], out_sem.at[k])
+
+    for k in range(SHIFT_MOST, SLOTS):
         out_ref[k] = conv[place(k - excess)]
+        give(k).start()
+    for k in range(SHIFT_MOST):
+        out_ref[k] = conv[place(k - excess)]
 
     @pl.when(jnp.logical_not(is_first))
     def _():
         tile.wait_recv()
+        late_at = [
+            jnp.minimum(k + SHIFT_MOST - jnp.clip(excess, 0, SHIFT_MOST), SHIFT_MOST - 1)
+            for k in range(SHIFT_MOST)
+        ]
         for k in range(SHIFT_MOST):
             own = out_ref[k].astype(jnp.float32)
-            theirs = arrived[k].astype(jnp.float32)
+            theirs = arrived[late_at[k]].astype(jnp.float32)
             late = jnp.full(own.shape, excess, jnp.int32) > k
             out_ref[k] = jnp.where(late, theirs, own).astype(jnp.bfloat16)
         up.wait_send()
 
+    for k in range(SHIFT_MOST):
+        give(k).start()
+
     @pl.when(jnp.logical_not(is_last))
     def _():
         down.wait_send()
@@ -235,6 +249,24 @@
         return carry
 
     lax.fori_loop(1, n, sent, 0)
+    for k in range(SLOTS):
+        give(k).wait()
+
+
+def hand_on(in_ref, out_ref, held, in_sem, out_sem):
+    def take(k):
+        return pltpu.make_async_copy(in_ref.at[k], held.at[k], in_sem.at[k])
+
+    def give(k):
+        return pltpu.make_async_copy(held.at[k], out_ref.at[k], out_sem.at[k])
+
+    for k in range(SLOTS):
+        take(k).start()
+    for k in range(SLOTS):
+        take(k).wait()
+        give(k).start()
+    for k in range(SLOTS):
+        give(k).wait()
 
 
 def on_device(slide_pixels, tissue_mask, conv_weight, conv_bias):
@@ -247,7 +279,7 @@
     quad = 2 * LANES
     vmem = pl.BlockSpec(memory_space=pltpu.VMEM)
     bf16 = jnp.bfloat16
-    return pl.pallas_call(
+    tiles = pl.pallas_call(
         functools.partial(kernel, n, side, channels),
         out_shape=jax.ShapeDtypeStruct((SLOTS, side, width), bf16),
         in_specs=[
@@ -255,7 +287,7 @@
             pl.BlockSpec(memory_space=pltpu.SMEM),
             vmem, vmem, vmem,
         ],
-        out_specs=vmem,
+        out_specs=pl.BlockSpec(memory_space=pl.ANY),
         scratch_shapes=[
             pltpu.VMEM((height + 2 * PACK, cols * width + 2 * LANES), bf16),
             pltpu.VMEM((band_rows * cols, side, width), bf16),
@@ -276,9 +308,22 @@
             pltpu.SemaphoreType.DMA((2,)),
             pltpu.SemaphoreType.DMA,
             pltpu.SemaphoreType.DMA,
+            pltpu.VMEM((SLOTS, side, width), bf16),
+            pltpu.SemaphoreType.DMA((SLOTS,)),
         ],
         compiler_params=pltpu.CompilerParams(collective_id=0, has_side_effects=True),
     )(slide_pixels, tissue_mask, tissue_mask, conv_weight, conv_bias.reshape(1, channels))
+    return pl.pallas_call(
+        hand_on,
+        out_shape=jax.ShapeDtypeStruct(tiles.shape, bf16),
+        in_specs=[pl.BlockSpec(memory_space=pl.ANY)],
+        out_specs=pl.BlockSpec(memory_space=pl.ANY),
+        scratch_shapes=[
+            pltpu.VMEM(tiles.shape, bf16),
+            pltpu.SemaphoreType.DMA((SLOTS,)),
+            pltpu.SemaphoreType.DMA((SLOTS,)),
+        ],
+    )(tiles)
 
 
 def solution(mesh):

time: 17.9 us -> 16.9 us (0.944)
  local copies, waits for them, and re-layouts: 2.3 us -> 0 us
  Pallas kernels: 15.3 us -> 16.7 us
    unnamed x1 -> x0, local copies, waits for them, and re-layouts: 2.3 us -> none
    pallas_call x0 -> x1, Pallas kernels: none -> 2.09 us  [on_device(): pl.pallas_call(hand_on, out_shape=jax.ShapeDtypeStruct(tiles.shape, bf16)...]
    pallas_call x1, Pallas kernels: 15.3 us -> 14.7 us  [on_device(): pl.pallas_call(functools.partial(kernel, n, side, channels), out_shape=ja...]
where the time goes in v2:
time: 16.9 us; the launch traced here: 16.8 us
  Pallas kernels  16.7 us (99%)
    pallas_call x1, Pallas kernels, on_device(): pl.pallas_call(functools.partial(kernel, n, side, channels), out_shape=ja...  14.7 us
    pallas_call x1, Pallas kernels, on_device(): pl.pallas_call(hand_on, out_shape=jax.ShapeDtypeStruct(tiles.shape, bf16)...  2.09 us

profile of v2, /device:TPU:8, one launch (start us, length us, event | category | flops | bytes accessed | tf_op | source)
XLA Modules:
  0.0 16.8 jit_solution(1938597655867210769)
XLA Ops:
  0.0 14.7 %shard_map.46.in_ref = bf16[8,32,2048]{2,1,0:T(8,128)(2,1)} custom-call(bf16[64,16384]{1,0:T(8,128)(2,1)} %x_ref.1, s32[2,8]{1,0:T(2,128)} %mask_v.1, s32[2,8]{1,0:T(2,128)} %mask_v.1, bf16[3,3,64,64]{3,2,1,0:T(8,128)(2,1)} %w_ref.1, bf16[1,64]{1,0:T(2,128)(2,1)} %bitcast.1), custom_call_target="tpu_custom_call" | custom-call | tf_op jit(solution)/shard_map/pallas_call | solution.py:282
  14.7 2.1 %shard_map.47 = bf16[8,32,2048]{2,1,0:T(8,128)(2,1)} custom-call(bf16[8,32,2048]{2,1,0:T(8,128)(2,1)} %shard_map.46.in_ref), custom_call_target="tpu_custom_call" | custom-call | tf_op jit(solution)/shard_map/pallas_call | solution.py:316

commit v3 on v2

--- a/solution.py
+++ b/solution.py
@@ -193,15 +193,17 @@
             total = total + jnp.where(count <= rank, 1, 0)
         return jnp.minimum(total, tiles - 1)
 
+    def tile(k):
+        return pltpu.make_async_remote_copy(
+            onward.at[k], arrived.at[k], tile_send.at[k], tile_recv.at[k],
+            device_id={"row": lax.rem(me + 1, n)}, device_id_type=MESH)
+
     for k in range(SHIFT_MOST):
         onward[k] = conv[place(seen[-1] - SHIFT_MOST + k)]
-    tile = pltpu.make_async_remote_copy(
-        onward, arrived, tile_send, tile_recv,
-        device_id={"row": lax.rem(me + 1, n)}, device_id_type=MESH)
-
-    @pl.when(jnp.logical_not(is_last))
-    def _():
-        tile.start()
+
+        @pl.when(jnp.logical_not(is_last))
+        def _():
+            tile(k).start()
 
     lax.fori_loop(0, duos - 1, functools.partial(convolve, 0), 0)
 
@@ -224,7 +226,8 @@
 
     @pl.when(jnp.logical_not(is_first))
     def _():
-        tile.wait_recv()
+        for k in range(SHIFT_MOST):
+            tile(k).wait_recv()
         late_at = [
             jnp.minimum(k + SHIFT_MOST - jnp.clip(excess, 0, SHIFT_MOST), SHIFT_MOST - 1)
             for k in range(SHIFT_MOST)
@@ -242,7 +245,8 @@
     @pl.when(jnp.logical_not(is_last))
     def _():
         down.wait_send()
-        tile.wait_send()
+        for k in range(SHIFT_MOST):
+            tile(k).wait_send()
 
     def sent(j, carry):
         mask_copy(lax.rem(me + j, n), me).wait_send()
@@ -306,8 +310,8 @@
             pltpu.SemaphoreType.DMA((n,)),
             pltpu.SemaphoreType.DMA((2,)),
             pltpu.SemaphoreType.DMA((2,)),
-            pltpu.SemaphoreType.DMA,
-            pltpu.SemaphoreType.DMA,
+            pltpu.SemaphoreType.DMA((SHIFT_MOST,)),
+            pltpu.SemaphoreType.DMA((SHIFT_MOST,)),
             pltpu.VMEM((SLOTS, side, width), bf16),
             pltpu.SemaphoreType.DMA((SLOTS,)),
         ],

time: 16.9 us -> 16.9 us (level)
  no operation moved by 1% of the time
where the time goes in v3:
time: 16.9 us; the launch traced here: 16.8 us
  Pallas kernels  16.8 us (99%)
    pallas_call x1, Pallas kernels, on_device(): pl.pallas_call(functools.partial(kernel, n, side, channels), out_shape=ja...  14.7 us
    pallas_call x1, Pallas kernels, on_device(): pl.pallas_call(hand_on, out_shape=jax.ShapeDtypeStruct(tiles.shape, bf16)...  2.09 us

profile of v3, /device:TPU:8, one launch (start us, length us, event | category | flops | bytes accessed | tf_op | source)
XLA Modules:
  0.0 16.8 jit_solution(2620445539030716302)
XLA Ops:
  0.0 14.7 %shard_map.46.in_ref = bf16[8,32,2048]{2,1,0:T(8,128)(2,1)} custom-call(bf16[64,16384]{1,0:T(8,128)(2,1)} %x_ref.1, s32[2,8]{1,0:T(2,128)} %mask_v.1, s32[2,8]{1,0:T(2,128)} %mask_v.1, bf16[3,3,64,64]{3,2,1,0:T(8,128)(2,1)} %w_ref.1, bf16[1,64]{1,0:T(2,128)(2,1)} %bitcast.1), custom_call_target="tpu_custom_call" | custom-call | tf_op jit(solution)/shard_map/pallas_call | solution.py:286
  14.7 2.1 %shard_map.47 = bf16[8,32,2048]{2,1,0:T(8,128)(2,1)} custom-call(bf16[8,32,2048]{2,1,0:T(8,128)(2,1)} %shard_map.46.in_ref), custom_call_target="tpu_custom_call" | custom-call | tf_op jit(solution)/shard_map/pallas_call | solution.py:320
